TPU v7x, 32 devices: a whole 2x2x4 slice. The times are simulated.
32 devices in a mesh: mem: 2 (over y), lat: 4 (over z), lon: 4 (over x, core).
Axes of the slice: x: 2, y: 2, z: 4, core: 2. Of those that a mesh axis runs over, the one named last changes fastest.
Arguments:
- control: bfloat16 [62, 3, 4, 4, 73728], P('mem', None, 'lat', 'lon'), may hold values from -6 to 6
- perturbs: bfloat16 [62, 3, 4, 4, 73728], P('mem', None, 'lat', 'lon'), may hold values from -0.75 to 0.75
- static_input: bfloat16 [3, 4, 4, 73728], P(None, 'lat', 'lon'), may hold values from -6 to 6
- lat_basis: bfloat16 [768, 384], replicated, may hold values from -0.21875 to 0.21875
- local_spectrum: float32 [384, 768], P(None, 'lat'), may hold values from 0.1 to 1
- static_spectrum: float32 [384, 768], P(None, 'lat'), may hold values from 0.1 to 1
- static_weight: float32 [3], replicated, may hold values from 0.2 to 0.8
Outputs:
- increment: float32 [3, 4, 4, 73728], P(None, 'lat', 'lon')
All inputs are finite; a program needn't handle non-finite values.
Results may differ from a plain program's by a relative error of at most 0.0073.
Values may be sent and summed in bfloat16 or wider, within the bound.
A program may use at most 128 MiB of HBM per device.

v0:
```python
import jax
import jax.numpy as jnp
from jax import lax
from jax.sharding import PartitionSpec as P

NLON = 1536
NLAT = 768
KLON = 768


def zonal_table():
    half = KLON // 2
    points = jnp.arange(NLON, dtype=jnp.int32)
    column = jnp.arange(KLON, dtype=jnp.int32)
    wave = jnp.where(column < half, column, column - half + 1)
    phase = points[:, None] * wave[None, :] % NLON
    angle = 2.0 * jnp.pi / NLON * phase.astype(jnp.float32)
    scale = jnp.sqrt(jnp.float32(2.0 / NLON))
    values = jnp.where(column[None, :] < half, jnp.cos(angle), jnp.sin(angle)) * scale
    return values.astype(jnp.bfloat16)


def shards(
    control, perturbs, static_input, lat_basis, local_spectrum, static_spectrum, static_weight
):
    mem_dev, levels = (control.shape[0], control.shape[1])
    cell_count = control.shape[-1]
    lat_rows = NLAT // lax.axis_size("lat")
    lon_cols = cell_count // lat_rows
    fields = jnp.concatenate([control, static_input[None]], 0).reshape(-1, lat_rows, lon_cols)
    per_lon = fields.shape[0] // lax.axis_size("lon")
    field_index = lax.axis_index("lon") * per_lon + jnp.arange(per_lon, dtype=jnp.int32)
    is_static = field_index >= mem_dev * levels
    first_mem = (lax.axis_index("mem") == 0).astype(jnp.float32)
    zonal = zonal_table()
    strips = lax.all_to_all(fields, "lon", split_axis=0, concat_axis=2, tiled=True)
    waves = jnp.einsum("bxn,nk->kbx", strips, zonal, preferred_element_type=jnp.float32).astype(
        jnp.bfloat16
    )
    merid = lax.all_to_all(waves, "lat", split_axis=0, concat_axis=2, tiled=True)
    coef = jnp.einsum("kby,yj->kbj", merid, lat_basis, preferred_element_type=jnp.float32)
    spectrum = jnp.where(
        is_static[None, :, None], static_spectrum.T[:, None, :], local_spectrum.T[:, None, :]
    )
    scaled = (coef * spectrum).astype(jnp.bfloat16)
    back = jnp.einsum("kbj,yj->kby", scaled, lat_basis, preferred_element_type=jnp.float32).astype(
        jnp.bfloat16
    )
    zonal_rows = lax.all_to_all(back, "lat", split_axis=2, concat_axis=0, tiled=True)
    grid = jnp.einsum("kbx,nk->bxn", zonal_rows, zonal, preferred_element_type=jnp.float32).astype(
        jnp.bfloat16
    )
    pert_fields = perturbs.reshape(mem_dev, levels, lat_rows, lon_cols)
    weight = static_weight[:, None, None]
    filtered = lax.all_to_all(grid, "lon", split_axis=2, concat_axis=0, tiled=True).reshape(
        mem_dev + 1, levels, lat_rows, lon_cols
    )
    ensemble = jnp.einsum(
        "mlxn,mlxn->lxn", pert_fields, filtered[:mem_dev], preferred_element_type=jnp.float32
    )
    static_part = filtered[mem_dev].astype(jnp.float32)
    own = first_mem * weight * static_part + (1.0 - weight) * ensemble
    total = lax.psum(own, "mem")
    return total.reshape(levels, 1, 1, cell_count)


def solution(mesh):
    return jax.shard_map(
        shards,
        mesh=mesh,
        in_specs=(
            P("mem", None, "lat", "lon", None),
            P("mem", None, "lat", "lon", None),
            P(None, "lat", "lon", None),
            P(),
            P(None, "lat"),
            P(None, "lat"),
            P(),
        ),
        out_specs=P(None, "lat", "lon", None),
        check_vma=False,
    )
```

profile of v0, /device:TPU:0, one launch (start us, length us, event | category | flops | bytes accessed | tf_op | source)
XLA Modules:
  0.0 1161.2 jit_solution(15015766370873050855)
XLA Ops:
  6.5 0.0 copy-start
  6.5 1.9 copy.44
  8.4 8.6 pad_maximum_fusion
  17.1 48.5 %copy.45 = bf16[32,3,1,1,73728]{4,1,0,3,2:T(4,128)(2,1)} copy(bf16[32,3,1,1,73728]{4,0,3,2,1:T(8,128)(2,1)S(1)} %pad_maximum_fusion) | data formatting | bytes 28311552 | tf_op jit(solution)/shard_map/concatenate | solution.py:30
  65.6 31.2 %reshape.38 = bf16[96,192,384]{2,1,0:T(8,128)(2,1)} reshape(bf16[32,3,1,1,73728]{4,1,0,3,2:T(4,128)(2,1)} %copy.45) | data formatting | bytes 28311552 | tf_op jit(solution)/shard_map/reshape | solution.py:30
  96.8 6.8 all-to-all-start
  103.7 19.8 %fusion.43 = bf16[1536,768,1]{1,0,2:T(8,128)(2,1)S(1)} fusion(s32[768]{0:T(1024)S(1)} %add_select_fusion.1, pred[768]{0:T(1024)(128)(4,1)S(1)} %iota_compare_fusion), kind=kLoop, calls=%fused_computation.21.clone.1.clone.1 | loop fusion | flops 14155776 | bytes 2363136 | tf_op jit(solution)/shard_map/bxn,nk->kbx/dot_general | solution.py:37
  123.5 135.9 %all-to-all-done = bf16[96,192,384]{2,1,0:T(8,128)(2,1)} async-done(((bf16[96,192,384]{2,1,0:T(8,128)(2,1)}), bf16[96,192,384]{2,1,0:T(8,128)(2,1)}, u32[]{:S(2)}, u32[]{:S(2)}) %all-to-all-start) | async-done | bytes 14155808 | tf_op jit(solution)/shard_map/all_to_all | solution.py:36
  259.4 10.6 copy.62
  270.0 16.3 %convolution_convert_fusion.2 = bf16[768,24,192]{0,2,1:T(8,128)(2,1)} fusion(bf16[24,192,1536]{2,1,0:T(8,128)(2,1)} %bitcast.63, bf16[1536,768,1]{1,0,2:T(8,128)(2,1)S(1)} %fusion.43), kind=kOutput, calls=%fused_computation.10 | convolution fusion | flops 10875174912 | bytes 23592960 | tf_op jit(solution)/shard_map/bxn,nk->kbx/dot_general | solution.py:37
  286.3 13.4 %copy.47 = bf16[768,24,192]{2,1,0:T(8,128)(2,1)} copy(bf16[768,24,192]{0,2,1:T(8,128)(2,1)} %convolution_convert_fusion.2) | data formatting | bytes 14155776 | tf_op jit(solution)/shard_map/convert_element_type | solution.py:37
  299.7 6.3 all-to-all-start.1
  306.1 206.2 %all-to-all-done.1 = bf16[768,24,192]{2,1,0:T(8,128)(2,1)} async-done(((bf16[768,24,192]{2,1,0:T(8,128)(2,1)}), bf16[768,24,192]{2,1,0:T(8,128)(2,1)}, u32[]{:S(2)}, u32[]{:S(2)}) %all-to-all-start.1) | async-done | bytes 7077920 | tf_op jit(solution)/shard_map/all_to_all | solution.py:40
  512.2 20.1 %copy.67 = bf16[4,192,24,192]{3,0,2,1:T(4,128)(2,1)} copy(bf16[4,192,24,192]{3,2,1,0:T(8,128)(2,1)} %bitcast.6) | data formatting | bytes 14155776 | tf_op jit(solution)/shard_map/all_to_all | solution.py:40
  532.3 0.0 copy-start.4
  532.3 0.0 copy-start.5
  532.3 16.6 %all_to_all.57 = bf16[192,24,768]{2,1,0:T(8,128)(2,1)} reshape(bf16[192,24,4,192]{3,2,1,0:T(4,128)(2,1)} %bitcast.61) | data formatting | bytes 14155776 | tf_op jit(solution)/shard_map/all_to_all | solution.py:40
  549.0 0.0 copy-done
  549.0 0.0 copy-done.4
  549.0 0.0 copy-done.5
  549.0 12.1 %convolution_convert_fusion.1 = bf16[192,24,768]{2,1,0:T(8,128)(2,1)} fusion(f32[192,384]{1,0:T(8,128)S(1)} %bitcast.65, f32[192,384]{1,0:T(8,128)S(1)} %bitcast.66, pred[24]{0:T(512)(128)(4,1)S(1)} %add_compare_fusion, bf16[192,24,768]{2,1,0:T(8,128)(2,1)} %all_to_all.57, bf16[768,384]{1,0:T(8,128)(2,1)S(1)} %copy-done), kind=kOutput, calls=%fused_computation.9 | convolution fusion | flops 5444665344 | bytes 15335448 | tf_op jit(solution)/shard_map/kbj,yj->kby/dot_general | solution.py:46
  561.1 13.5 %copy.49 = bf16[192,24,768]{0,1,2:T(8,128)(2,1)} copy(bf16[192,24,768]{2,1,0:T(8,128)(2,1)} %convolution_convert_fusion.1) | data formatting | bytes 14155776 | tf_op jit(solution)/shard_map/convert_element_type | solution.py:46
  574.6 6.0 all-to-all-start.2
  580.6 19.8 %fusion.41 = bf16[1536,768,1]{1,0,2:T(8,128)(2,1)S(1)} fusion(s32[768]{0:T(1024)S(1)} %add_select_fusion.1, pred[768]{0:T(1024)(128)(4,1)S(1)} %iota_compare_fusion), kind=kLoop, calls=%fused_computation.21.clone.clone.1 | loop fusion | flops 14155776 | bytes 2363136 | tf_op jit(solution)/shard_map/kbx,nk->bxn/dot_general | solution.py:50
  600.4 185.1 %all-to-all-done.2 = bf16[192,24,768]{0,1,2:T(8,128)(2,1)} async-done(((bf16[192,24,768]{0,1,2:T(8,128)(2,1)}), bf16[192,24,768]{0,1,2:T(8,128)(2,1)}, u32[]{:S(2)}, u32[]{:S(2)}) %all-to-all-start.2) | async-done | bytes 7077920 | tf_op jit(solution)/shard_map/all_to_all | solution.py:49
  785.5 13.5 %copy.66 = bf16[192,24,4,192]{0,2,3,1:T(4,128)(2,1)} copy(bf16[192,24,4,192]{0,1,3,2:T(8,128)(2,1)} %bitcast.11) | data formatting | bytes 14155776 | tf_op jit(solution)/shard_map/all_to_all | solution.py:49
  799.0 16.6 %all_to_all.61 = bf16[768,24,192]{0,2,1:T(8,128)(2,1)} reshape(bf16[4,192,24,192]{1,0,3,2:T(4,128)(2,1)} %bitcast.62) | data formatting | bytes 14155776 | tf_op jit(solution)/shard_map/all_to_all | solution.py:49
  815.6 16.9 %convolution_convert_fusion = bf16[24,192,1536]{2,1,0:T(8,128)(2,1)} fusion(bf16[768,24,192]{0,2,1:T(8,128)(2,1)} %all_to_all.61, bf16[1536,768,1]{1,0,2:T(8,128)(2,1)S(1)} %fusion.41), kind=kOutput, calls=%fused_computation.2 | convolution fusion | flops 10878713856 | bytes 23592960 | tf_op jit(solution)/shard_map/kbx,nk->bxn/dot_general | solution.py:50
  832.5 26.0 %copy.51 = bf16[24,192,1536]{1,0,2:T(8,128)(2,1)} copy(bf16[24,192,1536]{2,1,0:T(8,128)(2,1)} %convolution_convert_fusion) | data formatting | bytes 28311552 | tf_op jit(solution)/shard_map/convert_element_type | solution.py:50
  858.6 7.3 all-to-all-start.3
  865.9 0.0 copy-start.3
  865.9 0.3 all-reduce.2.cloned.1.call-start
  866.2 22.7 %reshape.40 = bf16[31,3,192,384]{3,2,0,1:T(8,128)(2,1)} reshape(bf16[31,3,1,1,73728]{4,0,3,2,1:T(8,128)(2,1)} %param.8) | data formatting | bytes 27426816 | tf_op jit(solution)/shard_map/reshape | solution.py:53
  888.9 0.0 copy-done.3
  889.0 182.5 %all-to-all-done.3 = bf16[24,192,1536]{1,0,2:T(8,128)(2,1)} async-done(((bf16[24,192,1536]{1,0,2:T(8,128)(2,1)}), bf16[24,192,1536]{1,0,2:T(8,128)(2,1)}, u32[]{:S(2)}, u32[]{:S(2)}) %all-to-all-start.3) | async-done | bytes 14155808 | tf_op jit(solution)/shard_map/all_to_all | solution.py:55
  1071.4 23.4 %copy.61 = bf16[24,192,4,384]{3,2,1,0:T(4,128)(2,1)} copy(bf16[24,192,4,384]{1,0,3,2:T(8,128)(2,1)} %bitcast.13) | data formatting | bytes 28311552 | tf_op jit(solution)/shard_map/all_to_all | solution.py:55
  1094.8 0.0 copy-start.2
  1094.8 8.5 copy.53
  1103.3 0.6 copy-done.2
  1103.9 0.0 copy-start.1
  1103.9 4.1 multiply_reduce_fusion
  1108.1 0.2 fusion.20
  1108.3 1.5 reshape.41
  1109.7 0.0 all-reduce.2.cloned.1.call-update
  1109.8 41.3 %all-reduce.2.cloned.1.call-done = f32[3,1,1,73728]{3,0,2,1:T(4,128)} async-done(((f32[3,1,1,73728]{3,0,2,1:T(4,128)}), f32[3,1,1,73728]{3,0,2,1:T(4,128)}) %all-reduce.2.cloned.1.call-update) | async-done | bytes 884752 | tf_op jit(solution)/shard_map/psum | solution.py:63
  1151.0 3.1 copy.54
  1154.1 0.0 copy-done.1
  (4 shorter events, 0.0 us)
Async XLA Ops:
  6.5 542.4 %copy-start = (bf16[768,384]{1,0:T(8,128)(2,1)S(1)}, bf16[768,384]{1,0:T(8,128)(2,1)}, u32[]{:S(2)}) copy-start(bf16[768,384]{1,0:T(8,128)(2,1)} %param.10) | copy-start | bytes 1769476
  96.8 162.6 %all-to-all-start = ((bf16[96,192,384]{2,1,0:T(8,128)(2,1)}), bf16[96,192,384]{2,1,0:T(8,128)(2,1)}, u32[]{:S(2)}, u32[]{:S(2)}) async-start(bf16[96,192,384]{2,1,0:T(8,128)(2,1)} %reshape.38), calls=%async_computation | async-start | bytes 28311552 | tf_op jit(solution)/shard_map/all_to_all | solution.py:36
  299.7 212.5 %all-to-all-start.1 = ((bf16[768,24,192]{2,1,0:T(8,128)(2,1)}), bf16[768,24,192]{2,1,0:T(8,128)(2,1)}, u32[]{:S(2)}, u32[]{:S(2)}) async-start(bf16[768,24,192]{2,1,0:T(8,128)(2,1)} %copy.47), calls=%async_computation.1 | async-start | bytes 18874368 | tf_op jit(solution)/shard_map/all_to_all | solution.py:40
  532.3 16.6 %copy-start.4 = (f32[384,192]{0,1:T(8,128)S(1)}, f32[384,192]{0,1:T(8,128)}, u32[]{:S(2)}) copy-start(f32[384,192]{0,1:T(8,128)} %param.11) | copy-start | bytes 884740
  532.3 16.6 %copy-start.5 = (f32[384,192]{0,1:T(8,128)S(1)}, f32[384,192]{0,1:T(8,128)}, u32[]{:S(2)}) copy-start(f32[384,192]{0,1:T(8,128)} %param.12) | copy-start | bytes 884740
  574.6 210.9 %all-to-all-start.2 = ((bf16[192,24,768]{0,1,2:T(8,128)(2,1)}), bf16[192,24,768]{0,1,2:T(8,128)(2,1)}, u32[]{:S(2)}, u32[]{:S(2)}) async-start(bf16[192,24,768]{0,1,2:T(8,128)(2,1)} %copy.49), calls=%async_computation.2 | async-start | bytes 18874368 | tf_op jit(solution)/shard_map/all_to_all | solution.py:49
  858.6 212.9 %all-to-all-start.3 = ((bf16[24,192,1536]{1,0,2:T(8,128)(2,1)}), bf16[24,192,1536]{1,0,2:T(8,128)(2,1)}, u32[]{:S(2)}, u32[]{:S(2)}) async-start(bf16[24,192,1536]{1,0,2:T(8,128)(2,1)} %copy.51), calls=%async_computation.3 | async-start | bytes 37748736 | tf_op jit(solution)/shard_map/all_to_all | solution.py:55
  865.9 23.0 %copy-start.3 = (f32[3]{0:T(128)S(1)}, f32[3]{0:T(128)}, u32[]{:S(2)}) copy-start(f32[3]{0:T(128)} %param.13) | copy-start | bytes 40
  865.9 285.1 %all-reduce.2.cloned.1.call-start = ((), (), s32[]{:S(2)}) async-start(), calls=%async_computation.4 | async-start | bytes 2359296 | tf_op jit(solution)/shard_map/psum | solution.py:63
  1094.8 9.2 copy-start.2
  1103.9 50.2 %copy-start.1 = (bf16[768,384]{1,0:T(8,128)(2,1)S(1)}, bf16[768,384]{1,0:T(8,128)(2,1)}, u32[]{:S(2)}) copy-start(bf16[768,384]{1,0:T(8,128)(2,1)} %param.10) | copy-start | bytes 1769476
Sparse Core Ops, SparseCore 0:
  1109.9 41.1 all-reduce.1
where the time goes:
time: 1170 us; the launch traced here: 1160 us
  waiting for transfers between devices  751 us (64%)
  local copies, waits for them, and re-layouts  272 us (23%)
  other arithmetic  52.6 us (4%)
  matrix products  45.4 us (4%)
  starting transfers between devices  26.8 us (2%)
  between operations  13.8 us (1%)
    all_to_all x1, waiting for transfers between devices, shards(): lax.all_to_all(waves, 'lat', split_axis=0, concat_axis=2, tiled=True)  206 us
    all_to_all x1, waiting for transfers between devices, shards(): lax.all_to_all(back, 'lat', split_axis=2, concat_axis=0, tiled=True)  185 us
    all_to_all x1, waiting for transfers between devices, shards(): lax.all_to_all(grid, 'lon', split_axis=2, concat_axis=0, tiled=True)  182 us
    all_to_all x1, waiting for transfers between devices, shards(): lax.all_to_all(fields, 'lon', split_axis=0, concat_axis=2, tiled=True)  136 us
    concatenate x1, local copies, waits for them, and re-layouts, shards(): jnp.concatenate([control, static_input[None]], 0)  48.5 us
    psum x1, waiting for transfers between devices, shards(): total = lax.psum(own, 'mem')  41.3 us
    all_to_all x2, local copies, waits for them, and re-layouts, shards(): lax.all_to_all(waves, 'lat', split_axis=0, concat_axis=2, tiled=True)  36.7 us
    all_to_all x2, local copies, waits for them, and re-layouts, shards(): lax.all_to_all(grid, 'lon', split_axis=2, concat_axis=0, tiled=True)  31.9 us
  transfers between devices with their start and end apart: 5, of which 5 were waited for; matrix products, arithmetic and copies ran while one was open for 5% of the time, Pallas kernels for 0%

commit v1 on v0

--- a/solution.py
+++ b/solution.py
@@ -6,6 +6,13 @@
 NLON = 1536
 NLAT = 768
 KLON = 768
+
+
+def stacked_exchange(x, name, split, join):
+    count = lax.axis_size(name)
+    shards = jnp.stack(jnp.split(x, count, axis=split), axis=0)
+    shards = lax.all_to_all(shards, name, split_axis=0, concat_axis=0)
+    return jnp.concatenate(shards, axis=join)
 
 
 def zonal_table():
@@ -52,9 +59,7 @@
     )
     pert_fields = perturbs.reshape(mem_dev, levels, lat_rows, lon_cols)
     weight = static_weight[:, None, None]
-    filtered = lax.all_to_all(grid, "lon", split_axis=2, concat_axis=0, tiled=True).reshape(
-        mem_dev + 1, levels, lat_rows, lon_cols
-    )
+    filtered = stacked_exchange(grid, "lon", 2, 0).reshape(mem_dev + 1, levels, lat_rows, lon_cols)
     ensemble = jnp.einsum(
         "mlxn,mlxn->lxn", pert_fields, filtered[:mem_dev], preferred_element_type=jnp.float32
     )

time: 1170 us -> 1070 us (0.915)
  waiting for transfers between devices: 751 us -> 693 us
  local copies, waits for them, and re-layouts: 272 us -> 219 us
  other arithmetic: 52.6 us -> 65.5 us
    all_to_all x1, waiting for transfers between devices: 182 us -> 132 us  [stacked_exchange(): shards = lax.all_to_all(shards, name, split_axis=0, concat_axis=0)]
    all_to_all x2 -> x0, local copies, waits for them, and re-layouts: 31.9 us -> none  [shards(): lax.all_to_all(grid, 'lon', split_axis=2, concat_axis=0, tiled=True)]
    convert_element_type x1 -> x0, local copies, waits for them, and re-layouts: 26 us -> none  [shards(): jnp.einsum('kbx,nk->bxn', zonal_rows, zonal, preferred_element_type=jnp.f...]
  transfers between devices with their start and end apart: 5 -> 5, of which waited for: 5 -> 5; matrix products, arithmetic and copies ran while one was open for 5% -> 6% of each run, Pallas kernels for 0% -> 0%
where the time goes in v1:
time: 1070 us; the launch traced here: 1060 us
  waiting for transfers between devices  693 us (65%)
  local copies, waits for them, and re-layouts  219 us (20%)
  other arithmetic  65.5 us (6%)
  matrix products  45.3 us (4%)
  starting transfers between devices  25.7 us (2%)
  between operations  13.5 us (1%)
    all_to_all x1, waiting for transfers between devices, shards(): lax.all_to_all(waves, 'lat', split_axis=0, concat_axis=2, tiled=True)  206 us
    all_to_all x1, waiting for transfers between devices, shards(): lax.all_to_all(back, 'lat', split_axis=2, concat_axis=0, tiled=True)  185 us
    all_to_all x1, waiting for transfers between devices, shards(): lax.all_to_all(fields, 'lon', split_axis=0, concat_axis=2, tiled=True)  136 us
    all_to_all x1, waiting for transfers between devices, stacked_exchange(): shards = lax.all_to_all(shards, name, split_axis=0, concat_axis=0)  132 us
    concatenate x1, local copies, waits for them, and re-layouts, shards(): jnp.concatenate([control, static_input[None]], 0)  48.5 us
    all_to_all x2, local copies, waits for them, and re-layouts, shards(): lax.all_to_all(waves, 'lat', split_axis=0, concat_axis=2, tiled=True)  36.7 us
    psum x1, waiting for transfers between devices, shards(): total = lax.psum(own, 'mem')  34.8 us
    reshape x1, local copies, waits for them, and re-layouts, shards(): jnp.concatenate([control, static_input[None]], 0)  31.2 us
  transfers between devices with their start and end apart: 5, of which 5 were waited for; matrix products, arithmetic and copies ran while one was open for 6% of the time, Pallas kernels for 0%

profile of v1, /device:TPU:0, one launch (start us, length us, event | category | flops | bytes accessed | tf_op | source)
XLA Modules:
  0.0 1062.5 jit_solution(9279485750616114646)
XLA Ops:
  6.5 0.0 copy-start
  6.5 1.9 copy.22
  8.4 8.6 pad_maximum_fusion
  17.1 48.5 %copy.23 = bf16[32,3,1,1,73728]{4,1,0,3,2:T(4,128)(2,1)} copy(bf16[32,3,1,1,73728]{4,0,3,2,1:T(8,128)(2,1)S(1)} %pad_maximum_fusion) | data formatting | bytes 28311552 | tf_op jit(solution)/shard_map/concatenate | solution.py:37
  65.6 31.2 %reshape.34 = bf16[96,192,384]{2,1,0:T(8,128)(2,1)} reshape(bf16[32,3,1,1,73728]{4,1,0,3,2:T(4,128)(2,1)} %copy.23) | data formatting | bytes 28311552 | tf_op jit(solution)/shard_map/reshape | solution.py:37
  96.8 6.7 all-to-all-start
  103.6 19.8 %fusion.43 = bf16[1536,768,1]{1,0,2:T(8,128)(2,1)S(1)} fusion(s32[768]{0:T(1024)S(1)} %add_select_fusion.1, pred[768]{0:T(1024)(128)(4,1)S(1)} %iota_compare_fusion), kind=kLoop, calls=%fused_computation.26.clone.1.clone.1 | loop fusion | flops 14155776 | bytes 2363136 | tf_op jit(solution)/shard_map/bxn,nk->kbx/dot_general | solution.py:44
  123.4 135.9 %all-to-all-done = bf16[96,192,384]{2,1,0:T(8,128)(2,1)} async-done(((bf16[96,192,384]{2,1,0:T(8,128)(2,1)}), bf16[96,192,384]{2,1,0:T(8,128)(2,1)}, u32[]{:S(2)}, u32[]{:S(2)}) %all-to-all-start) | async-done | bytes 14155808 | tf_op jit(solution)/shard_map/all_to_all | solution.py:43
  259.3 10.6 %copy.35 = bf16[4,24,24,8,384]{4,3,0,2,1:T(8,128)(2,1)} copy(bf16[4,24,24,8,384]{4,3,2,1,0:T(8,128)(2,1)} %bitcast.21) | data formatting | bytes 28311552 | tf_op jit(solution)/shard_map/all_to_all | solution.py:43
  269.9 16.3 %convolution_convert_fusion.2 = bf16[768,24,192]{0,2,1:T(8,128)(2,1)} fusion(bf16[24,192,1536]{2,1,0:T(8,128)(2,1)} %bitcast.66, bf16[1536,768,1]{1,0,2:T(8,128)(2,1)S(1)} %fusion.43), kind=kOutput, calls=%fused_computation.11 | convolution fusion | flops 10875174912 | bytes 23592960 | tf_op jit(solution)/shard_map/bxn,nk->kbx/dot_general | solution.py:44
  286.2 13.4 %copy.25 = bf16[768,24,192]{2,1,0:T(8,128)(2,1)} copy(bf16[768,24,192]{0,2,1:T(8,128)(2,1)} %convolution_convert_fusion.2) | data formatting | bytes 14155776 | tf_op jit(solution)/shard_map/convert_element_type | solution.py:44
  299.6 6.0 all-to-all-start.1
  305.7 206.0 %all-to-all-done.1 = bf16[768,24,192]{2,1,0:T(8,128)(2,1)} async-done(((bf16[768,24,192]{2,1,0:T(8,128)(2,1)}), bf16[768,24,192]{2,1,0:T(8,128)(2,1)}, u32[]{:S(2)}, u32[]{:S(2)}) %all-to-all-start.1) | async-done | bytes 7077920 | tf_op jit(solution)/shard_map/all_to_all | solution.py:47
  511.7 20.1 %copy.40 = bf16[4,192,24,192]{3,0,2,1:T(4,128)(2,1)} copy(bf16[4,192,24,192]{3,2,1,0:T(8,128)(2,1)} %bitcast.6) | data formatting | bytes 14155776 | tf_op jit(solution)/shard_map/all_to_all | solution.py:47
  531.8 0.0 copy-start.3
  531.8 0.0 copy-start.4
  531.8 16.6 %all_to_all.49 = bf16[192,24,768]{2,1,0:T(8,128)(2,1)} reshape(bf16[192,24,4,192]{3,2,1,0:T(4,128)(2,1)} %bitcast.64) | data formatting | bytes 14155776 | tf_op jit(solution)/shard_map/all_to_all | solution.py:47
  548.4 0.0 copy-done
  548.4 0.0 copy-done.3
  548.4 0.0 copy-done.4
  548.4 12.1 %convolution_convert_fusion.1 = bf16[192,24,768]{2,1,0:T(8,128)(2,1)} fusion(f32[192,384]{1,0:T(8,128)S(1)} %bitcast.68, f32[192,384]{1,0:T(8,128)S(1)} %bitcast.69, pred[24]{0:T(512)(128)(4,1)S(1)} %add_compare_fusion, bf16[192,24,768]{2,1,0:T(8,128)(2,1)} %all_to_all.49, bf16[768,384]{1,0:T(8,128)(2,1)S(1)} %copy-done), kind=kOutput, calls=%fused_computation.10 | convolution fusion | flops 5444665344 | bytes 15335448 | tf_op jit(solution)/shard_map/kbj,yj->kby/dot_general | solution.py:53
  560.5 13.5 %copy.27 = bf16[192,24,768]{0,1,2:T(8,128)(2,1)} copy(bf16[192,24,768]{2,1,0:T(8,128)(2,1)} %convolution_convert_fusion.1) | data formatting | bytes 14155776 | tf_op jit(solution)/shard_map/convert_element_type | solution.py:53
  574.0 6.1 all-to-all-start.2
  580.1 19.8 %fusion.41 = bf16[1536,768,1]{1,0,2:T(8,128)(2,1)S(1)} fusion(s32[768]{0:T(1024)S(1)} %add_select_fusion.1, pred[768]{0:T(1024)(128)(4,1)S(1)} %iota_compare_fusion), kind=kLoop, calls=%fused_computation.26.clone.clone.1 | loop fusion | flops 14155776 | bytes 2363136 | tf_op jit(solution)/shard_map/kbx,nk->bxn/dot_general | solution.py:57
  599.9 184.9 %all-to-all-done.2 = bf16[192,24,768]{0,1,2:T(8,128)(2,1)} async-done(((bf16[192,24,768]{0,1,2:T(8,128)(2,1)}), bf16[192,24,768]{0,1,2:T(8,128)(2,1)}, u32[]{:S(2)}, u32[]{:S(2)}) %all-to-all-start.2) | async-done | bytes 7077920 | tf_op jit(solution)/shard_map/all_to_all | solution.py:56
  784.8 13.5 %copy.39 = bf16[192,24,4,192]{0,2,3,1:T(4,128)(2,1)} copy(bf16[192,24,4,192]{0,1,3,2:T(8,128)(2,1)} %bitcast.11) | data formatting | bytes 14155776 | tf_op jit(solution)/shard_map/all_to_all | solution.py:56
  798.3 16.6 %all_to_all.53 = bf16[768,24,192]{0,2,1:T(8,128)(2,1)} reshape(bf16[4,192,24,192]{1,0,3,2:T(4,128)(2,1)} %bitcast.65) | data formatting | bytes 14155776 | tf_op jit(solution)/shard_map/all_to_all | solution.py:56
  814.8 16.9 %convolution_convert_fusion = bf16[24,192,1536]{2,1,0:T(8,128)(2,1)} fusion(bf16[768,24,192]{0,2,1:T(8,128)(2,1)} %all_to_all.53, bf16[1536,768,1]{1,0,2:T(8,128)(2,1)S(1)} %fusion.41), kind=kOutput, calls=%fused_computation.3 | convolution fusion | flops 10878713856 | bytes 23592960 | tf_op jit(solution)/shard_map/kbx,nk->bxn/dot_general | solution.py:57
  831.8 6.1 slice_bitcast_fusion.4
  837.9 5.3 pad_maximum_fusion.1
  843.2 6.6 all-to-all-start.3
  849.8 0.0 copy-start.2
  849.8 0.3 all-reduce.2.cloned.1.call-start
  850.1 22.8 %reshape.35 = bf16[31,3,192,384]{3,2,0,1:T(8,128)(2,1)} reshape(bf16[31,3,1,1,73728]{4,0,3,2,1:T(8,128)(2,1)} %param.8) | data formatting | bytes 27426816 | tf_op jit(solution)/shard_map/reshape | solution.py:60
  872.9 0.0 copy-done.2
  872.9 131.8 %all-to-all-done.3 = bf16[4,24,192,384]{3,2,1,0:T(8,128)(2,1)} async-done(((bf16[4,24,192,384]{3,2,1,0:T(8,128)(2,1)}), bf16[4,24,192,384]{3,2,1,0:T(8,128)(2,1)}, u32[]{:S(2)}, u32[]{:S(2)}) %all-to-all-start.3) | async-done | bytes 14155808 | tf_op jit(solution)/shard_map/all_to_all | solution.py:14
  1004.7 0.0 copy-start.1
  1004.7 10.7 %multiply_reduce_fusion = f32[3,192,384]{2,1,0:T(8,128)S(1)} fusion(bf16[31,3,192,384]{3,2,0,1:T(8,128)(2,1)} %reshape.35, bf16[32,3,192,384]{3,2,1,0:T(8,128)(2,1)} %bitcast.17), kind=kLoop, calls=%fused_computation | loop fusion | flops 27205632 | bytes 28311552 | tf_op jit(solution)/shard_map/mlxn,mlxn->lxn/dot_general | solution.py:63
  1015.4 1.2 fusion.20
  1016.6 2.0 reshape.36
  1018.6 0.0 all-reduce.2.cloned.1.call-update
  1018.7 34.8 %all-reduce.2.cloned.1.call-done = f32[3,1,1,73728]{3,2,1,0:T(1,128)} async-done(((f32[3,1,1,73728]{3,2,1,0:T(1,128)}), f32[3,1,1,73728]{3,2,1,0:T(1,128)}) %all-reduce.2.cloned.1.call-update) | async-done | bytes 884752 | tf_op jit(solution)/shard_map/psum | solution.py:68
  1053.5 2.1 copy.42
  1055.6 0.0 copy-done.1
  (4 shorter events, 0.0 us)
Async XLA Ops:
  6.5 541.9 %copy-start = (bf16[768,384]{1,0:T(8,128)(2,1)S(1)}, bf16[768,384]{1,0:T(8,128)(2,1)}, u32[]{:S(2)}) copy-start(bf16[768,384]{1,0:T(8,128)(2,1)} %param.10) | copy-start | bytes 1769476
  96.8 162.5 %all-to-all-start = ((bf16[96,192,384]{2,1,0:T(8,128)(2,1)}), bf16[96,192,384]{2,1,0:T(8,128)(2,1)}, u32[]{:S(2)}, u32[]{:S(2)}) async-start(bf16[96,192,384]{2,1,0:T(8,128)(2,1)} %reshape.34), calls=%async_computation | async-start | bytes 28311552 | tf_op jit(solution)/shard_map/all_to_all | solution.py:43
  299.6 212.1 %all-to-all-start.1 = ((bf16[768,24,192]{2,1,0:T(8,128)(2,1)}), bf16[768,24,192]{2,1,0:T(8,128)(2,1)}, u32[]{:S(2)}, u32[]{:S(2)}) async-start(bf16[768,24,192]{2,1,0:T(8,128)(2,1)} %copy.25), calls=%async_computation.1 | async-start | bytes 18874368 | tf_op jit(solution)/shard_map/all_to_all | solution.py:47
  531.8 16.6 %copy-start.3 = (f32[384,192]{0,1:T(8,128)S(1)}, f32[384,192]{0,1:T(8,128)}, u32[]{:S(2)}) copy-start(f32[384,192]{0,1:T(8,128)} %param.11) | copy-start | bytes 884740
  531.8 16.6 %copy-start.4 = (f32[384,192]{0,1:T(8,128)S(1)}, f32[384,192]{0,1:T(8,128)}, u32[]{:S(2)}) copy-start(f32[384,192]{0,1:T(8,128)} %param.12) | copy-start | bytes 884740
  574.0 210.8 %all-to-all-start.2 = ((bf16[192,24,768]{0,1,2:T(8,128)(2,1)}), bf16[192,24,768]{0,1,2:T(8,128)(2,1)}, u32[]{:S(2)}, u32[]{:S(2)}) async-start(bf16[192,24,768]{0,1,2:T(8,128)(2,1)} %copy.27), calls=%async_computation.2 | async-start | bytes 18874368 | tf_op jit(solution)/shard_map/all_to_all | solution.py:56
  843.2 161.5 %all-to-all-start.3 = ((bf16[4,24,192,384]{3,2,1,0:T(8,128)(2,1)}), bf16[4,24,192,384]{3,2,1,0:T(8,128)(2,1)}, u32[]{:S(2)}, u32[]{:S(2)}) async-start(bf16[4,24,192,384]{3,2,1,0:T(8,128)(2,1)} %pad_maximum_fusion.1), calls=%async_computation.3 | async-start | bytes 28311552 | tf_op jit(solution)/shard_map/all_to_all | solution.py:14
  849.8 23.1 %copy-start.2 = (f32[3]{0:T(128)S(1)}, f32[3]{0:T(128)}, u32[]{:S(2)}) copy-start(f32[3]{0:T(128)} %param.13) | copy-start | bytes 40
  849.8 203.7 %all-reduce.2.cloned.1.call-start = ((), (), s32[]{:S(2)}) async-start(), calls=%async_computation.4 | async-start | bytes 1769472 | tf_op jit(solution)/shard_map/psum | solution.py:68
  1004.7 50.9 %copy-start.1 = (bf16[768,384]{1,0:T(8,128)(2,1)S(1)}, bf16[768,384]{1,0:T(8,128)(2,1)}, u32[]{:S(2)}) copy-start(bf16[768,384]{1,0:T(8,128)(2,1)} %param.10) | copy-start | bytes 1769476
Sparse Core Ops, SparseCore 0:
  1018.8 34.6 all-reduce.1
